TPU v7x, 32 devices: a whole 2x2x4 slice. The times are simulated.
32 devices in a mesh: row: 4 (over y, x), col: 4 (over z), depth: 2 (over core).
Axes of the slice: x: 2, y: 2, z: 4, core: 2. Of those that a mesh axis runs over, the one named last changes fastest.
Arguments:
- layers: float32 [2, 4096, 4096], P('depth', 'row', 'col'), may hold values from -3 to 134.2, as said below
Outputs:
- factor: float32 [2, 4096, 512], P(None, 'row', 'depth')
- schur: float32 [4096, 4096], P(('row', 'depth'), 'col')
Inputs may be any that keep to these rules, and one draw needn't show every extreme that they name: Read in matrix order, each layer is symmetric, and the sum over layers is symmetric positive definite with a diagonal of order sqrt(4096).
All inputs are finite; a program needn't handle non-finite values.
Results may differ from a plain program's by a relative error of at most 0.0001.
Values sent between devices are 32-bit elements; how exact they have to be, the bound alone decides.
A program may use at most 192 MiB of HBM per device.

v0:
```python
import jax
import jax.numpy as jnp
from jax import lax
from jax.sharding import PartitionSpec as P

PANEL = 512
PANELS = 2


def broadcast(value, axis, source):
    kept = jnp.where(lax.axis_index(axis) == source, value, 0).astype(value.dtype)
    return lax.psum(kept, axis)


def block_inverse(diagonal, identity_block):
    lower_diag = jnp.linalg.cholesky(diagonal)
    return jax.scipy.linalg.solve_triangular(lower_diag, identity_block, lower=True)


def outer_update(left_rows, right_rows):
    return lax.dot_general(
        left_rows,
        right_rows,
        (((1,), (1,)), ((), ())),
        precision=lax.Precision.HIGHEST,
        preferred_element_type=jnp.float32,
    )


def per_device(layers):
    row_groups = lax.axis_size("row")
    col_groups = lax.axis_size("col")
    depth_groups = lax.axis_size("depth")
    row_index = lax.axis_index("row")
    col_index = lax.axis_index("col")
    depth_index = lax.axis_index("depth")
    layer_part = layers[0]
    rows_local = layer_part.shape[0]
    cols_local = layer_part.shape[1]
    slice_width = PANEL // depth_groups
    quarter_rows = rows_local // depth_groups
    local_blocks = rows_local // PANEL
    row_block = jnp.arange(rows_local, dtype=jnp.int32) // PANEL * row_groups + row_index
    col_block = jnp.arange(cols_local, dtype=jnp.int32) // PANEL * col_groups + col_index
    identity_block = jnp.eye(PANEL, dtype=jnp.float32)
    factor_list = []
    schur = None
    for panel_step in range(PANELS):
        owner_col = panel_step % col_groups
        local_col = panel_step // col_groups
        owner_row = panel_step % row_groups
        local_row = panel_step // row_groups
        column = layer_part[:, local_col * PANEL : (local_col + 1) * PANEL]
        layer_diag = broadcast(
            column[local_row * PANEL : (local_row + 1) * PANEL], "row", owner_row
        )
        diagonal = lax.psum(layer_diag, "depth")
        quarter = lax.psum_scatter(column, "depth", scatter_dimension=0, tiled=True)
        inverse = block_inverse(diagonal, identity_block)
        solved = jnp.dot(quarter, inverse.T, precision=lax.Precision.HIGHEST)
        quarter_block = lax.dynamic_slice_in_dim(
            row_block, depth_index * quarter_rows, quarter_rows, 0
        )
        solved = jnp.where(quarter_block[:, None] >= panel_step, solved, 0.0)
        row_slice = lax.all_to_all(solved, "depth", split_axis=1, concat_axis=0, tiled=True)
        panel_rows = broadcast(row_slice, "col", owner_col)
        factor_list.append(panel_rows)
        update_rows = jnp.where(row_block[:, None] > panel_step, panel_rows, 0.0)
        gathered = lax.all_gather(panel_rows, "row", axis=0, tiled=True)
        grouped = gathered.reshape(
            row_groups // col_groups, col_groups, local_blocks, PANEL, slice_width
        )
        picked = lax.dynamic_index_in_dim(grouped, col_index, 1, keepdims=False)
        column_rows = picked.transpose(1, 0, 2, 3).reshape(cols_local, slice_width)
        update_cols = jnp.where(col_block[:, None] > panel_step, column_rows, 0.0)
        if panel_step + 1 < PANELS:
            layer_part = layer_part - outer_update(update_rows, update_cols)
        else:
            schur = lax.psum_scatter(
                layer_part - outer_update(update_rows, update_cols),
                "depth",
                scatter_dimension=0,
                tiled=True,
            )
    return (jnp.stack(factor_list), schur)


def solution(mesh):
    return jax.shard_map(
        per_device,
        mesh=mesh,
        in_specs=(P("depth", "row", "col"),),
        out_specs=(P(None, "row", "depth"), P(("row", "depth"), "col")),
        check_vma=False,
    )
```

profile of v0, /device:TPU:31, one launch (start us, length us, event | category | flops | bytes accessed | tf_op | source)
XLA Modules:
  0.0 726.9 jit_solution(16254621082217000149)
XLA Ops:
  14.9 52.4 %all-reduce.8.cloned.1.call-done = f32[512,512]{0,1:T(8,128)} async-done(((f32[512,512]{0,1:T(8,128)}), f32[512,512]{0,1:T(8,128)}) %all-reduce.8.cloned.1.call-update) | async-done | bytes 1048592 | tf_op jit(solution)/shard_map/psum | solution.py:12
  70.9 20.1 %all-reduce.10.cloned.1.call-done = f32[512,512]{0,1:T(8,128)} async-done(((f32[512,512]{0,1:T(8,128)}), f32[512,512]{0,1:T(8,128)}) %all-reduce.10.cloned.1.call-update) | async-done | bytes 1048592 | tf_op jit(solution)/shard_map/psum | solution.py:57
  94.0 11.7 %cholesky.286 = f32[128,128]{1,0:T(8,128)S(1)} custom-call(f32[128,128]{1,0:T(8,128)S(1)} %cholesky.426), custom_call_target="Cholesky" | custom-call | tf_op jit(solution)/shard_map/jit(cholesky)/cholesky | solution.py:16
  116.3 11.7 %cholesky.305 = f32[128,128]{1,0:T(8,128)S(1)} custom-call(f32[128,128]{1,0:T(8,128)S(1)} %cholesky.430), custom_call_target="Cholesky" | custom-call | tf_op jit(solution)/shard_map/jit(cholesky)/cholesky | solution.py:16
  128.1 10.0 %custom-call.28 = f32[1,128,128]{1,2,0:T(8,128)S(1)} custom-call(f32[1,128,128]{2,1,0:T(8,128)S(1)} %get-tuple-element.58), custom_call_target="InvertDiagBlocksLowerTriangular" | custom-call | tf_op jit(solution)/shard_map/jit(cholesky)/cholesky | solution.py:16
  138.7 11.7 %cholesky.326 = f32[128,128]{1,0:T(8,128)S(1)} custom-call(f32[128,128]{1,0:T(8,128)S(1)} %cholesky.435), custom_call_target="Cholesky" | custom-call | tf_op jit(solution)/shard_map/jit(cholesky)/cholesky | solution.py:16
  150.5 9.8 %custom-call.29 = f32[1,128,128]{1,2,0:T(8,128)S(1)} custom-call(f32[1,128,128]{2,1,0:T(8,128)S(1)} %get-tuple-element.55), custom_call_target="InvertDiagBlocksLowerTriangular" | custom-call | tf_op jit(solution)/shard_map/jit(cholesky)/cholesky | solution.py:16
  160.9 11.7 %cholesky.343 = f32[128,128]{1,0:T(8,128)S(1)} custom-call(f32[128,128]{1,0:T(8,128)S(1)} %convolution_subtract_fusion.13), custom_call_target="Cholesky" | custom-call | tf_op jit(solution)/shard_map/jit(cholesky)/cholesky | solution.py:16
  185.9 39.3 %custom-call.30 = f32[4,128,128]{1,2,0:T(8,128)S(1)} custom-call(f32[4,128,128]{2,1,0:T(8,128)S(1)} %get-tuple-element.18), custom_call_target="InvertDiagBlocksLowerTriangular" | custom-call | tf_op jit(solution)/shard_map/jit(_solve_triangular)/triangular_solve | solution.py:17
  240.7 51.1 %all-reduce.12.cloned.1.call-done = f32[1024,256]{1,0:T(8,128)} async-done(((f32[1024,256]{1,0:T(8,128)}), f32[1024,256]{1,0:T(8,128)}) %all-reduce.12.cloned.1.call-update) | async-done | bytes 1048592 | tf_op jit(solution)/shard_map/psum | solution.py:12
  291.9 53.9 %all-gather.3.cloned.1.call-done = f32[4096,256]{1,0:T(8,128)} async-done(((f32[1024,256]{1,0:T(8,128)}), f32[4096,256]{1,0:T(8,128)}) %all-gather.3.cloned.1.call-update) | async-done | bytes 4194320 | tf_op jit(solution)/shard_map/all_gather | solution.py:69
  355.3 52.6 %all-reduce.14.cloned.1.call-done = f32[512,512]{0,1:T(8,128)} async-done(((f32[512,512]{0,1:T(8,128)}), f32[512,512]{0,1:T(8,128)}) %all-reduce.14.cloned.1.call-update) | async-done | bytes 1048592 | tf_op jit(solution)/shard_map/psum | solution.py:12
  411.3 20.1 %all-reduce.16.cloned.1.call-done = f32[512,512]{0,1:T(8,128)} async-done(((f32[512,512]{0,1:T(8,128)}), f32[512,512]{0,1:T(8,128)}) %all-reduce.16.cloned.1.call-update) | async-done | bytes 1048592 | tf_op jit(solution)/shard_map/psum | solution.py:57
  435.4 11.7 %cholesky.358 = f32[128,128]{1,0:T(8,128)S(1)} custom-call(f32[128,128]{1,0:T(8,128)S(1)} %cholesky.439), custom_call_target="Cholesky" | custom-call | tf_op jit(solution)/shard_map/jit(cholesky)/cholesky | solution.py:16
  459.6 11.7 %cholesky.377 = f32[128,128]{1,0:T(8,128)S(1)} custom-call(f32[128,128]{1,0:T(8,128)S(1)} %cholesky.443), custom_call_target="Cholesky" | custom-call | tf_op jit(solution)/shard_map/jit(cholesky)/cholesky | solution.py:16
  471.4 10.0 %custom-call.32 = f32[1,128,128]{1,2,0:T(8,128)S(1)} custom-call(f32[1,128,128]{2,1,0:T(8,128)S(1)} %get-tuple-element.48), custom_call_target="InvertDiagBlocksLowerTriangular" | custom-call | tf_op jit(solution)/shard_map/jit(cholesky)/cholesky | solution.py:16
  483.0 11.7 %cholesky.398 = f32[128,128]{1,0:T(8,128)S(1)} custom-call(f32[128,128]{1,0:T(8,128)S(1)} %cholesky.448), custom_call_target="Cholesky" | custom-call | tf_op jit(solution)/shard_map/jit(cholesky)/cholesky | solution.py:16
  494.7 9.8 %custom-call.33 = f32[1,128,128]{1,2,0:T(8,128)S(1)} custom-call(f32[1,128,128]{2,1,0:T(8,128)S(1)} %get-tuple-element.45), custom_call_target="InvertDiagBlocksLowerTriangular" | custom-call | tf_op jit(solution)/shard_map/jit(cholesky)/cholesky | solution.py:16
  506.0 11.7 %cholesky.415 = f32[128,128]{1,0:T(8,128)S(1)} custom-call(f32[128,128]{1,0:T(8,128)S(1)} %convolution_subtract_fusion.12), custom_call_target="Cholesky" | custom-call | tf_op jit(solution)/shard_map/jit(cholesky)/cholesky | solution.py:16
  524.2 11.7 %while.5 = (s32[]{:T(128)}, f32[512,512]{1,0:T(8,128)}, s32[4,2]{0,1:T(2,128)S(1)}, f32[4,128,128]{2,1,0:T(8,128)S(1)}, s32[]{:T(128)}) while((s32[]{:T(128)}, f32[512,512]{1,0:T(8,128)}, s32[4,2]{0,1:T(2,128)S(1)}, f32[4,128,128]{2,1,0:T(8,128)S(1)}, s32[]{:T(128)}) %tuple.85), condition=%wide.while_cond.clone, body=%wide.while_body.clone.sunk | while | flops 2 | bytes 131181 | solution.py:17
  536.0 39.3 %custom-call.34 = f32[4,128,128]{1,2,0:T(8,128)S(1)} custom-call(f32[4,128,128]{2,1,0:T(8,128)S(1)} %get-tuple-element.19), custom_call_target="InvertDiagBlocksLowerTriangular" | custom-call | tf_op jit(solution)/shard_map/jit(_solve_triangular)/triangular_solve | solution.py:17
  590.2 51.1 %all-reduce.18.cloned.1.call-done = f32[1024,256]{1,0:T(8,128)} async-done(((f32[1024,256]{1,0:T(8,128)}), f32[1024,256]{1,0:T(8,128)}) %all-reduce.18.cloned.1.call-update) | async-done | bytes 1048592 | tf_op jit(solution)/shard_map/psum | solution.py:12
  641.3 53.9 %all-gather.5.cloned.1.call-done = f32[4096,256]{1,0:T(8,128)} async-done(((f32[1024,256]{1,0:T(8,128)}), f32[4096,256]{1,0:T(8,128)}) %all-gather.5.cloned.1.call-update) | async-done | bytes 4194320 | tf_op jit(solution)/shard_map/all_gather | solution.py:69
  704.7 12.4 %reduce-scatter.8.cloned.1.call-done = f32[512,1024]{0,1:T(8,128)} async-done(((f32[1024,1024]{0,1:T(8,128)}), f32[512,1024]{0,1:T(8,128)}) %reduce-scatter.8.cloned.1.call-update) | async-done | bytes 2097168 | tf_op jit(solution)/shard_map/reduce_scatter | solution.py:79
  (153 shorter events, 135.5 us)
Async XLA Ops:
  7.2 60.2 %all-reduce.8.cloned.1.call-start = ((), (), s32[]{:S(2)}) async-start(), calls=%async_computation.5 | async-start | bytes 2097152 | tf_op jit(solution)/shard_map/psum | solution.py:12
  14.9 76.1 %all-reduce.10.cloned.1.call-start = ((), (), s32[]{:S(2)}) async-start(), calls=%async_computation.6 | async-start | bytes 2097152 | tf_op jit(solution)/shard_map/psum | solution.py:57
  67.3 162.0 %reduce-scatter.4.cloned.1.call-start = ((), (), s32[]{:S(2)}) async-start(), calls=%async_computation.7 | async-start | bytes 3145728 | tf_op jit(solution)/shard_map/reduce_scatter | solution.py:58
  70.6 221.2 %all-reduce.12.cloned.1.call-start = ((), (), s32[]{:S(2)}) async-start(), calls=%async_computation.8 | async-start | bytes 2097152 | tf_op jit(solution)/shard_map/psum | solution.py:12
  225.3 2.1 copy-start.6
  240.7 105.1 %all-gather.3.cloned.1.call-start = ((), (), s32[]{:S(2)}) async-start(), calls=%async_computation.9 | async-start | bytes 5242880 | tf_op jit(solution)/shard_map/all_gather | solution.py:69
  291.8 55.7 %copy-start.3 = (f32[1024,256]{1,0:T(8,128)S(1)}, f32[1024,256]{1,0:T(8,128)}, u32[]{:S(2)}) copy-start(f32[1024,256]{1,0:T(8,128)} %all-reduce.12.cloned.1.call-done) | copy-start | bytes 3145732
  291.8 116.0 %all-reduce.14.cloned.1.call-start = ((), (), s32[]{:S(2)}) async-start(), calls=%async_computation.11 | async-start | bytes 2097152 | tf_op jit(solution)/shard_map/psum | solution.py:12
  345.8 2.5 copy-start
  352.2 1.9 copy-start.1
  355.2 76.2 %all-reduce.16.cloned.1.call-start = ((), (), s32[]{:S(2)}) async-start(), calls=%async_computation.12 | async-start | bytes 2097152 | tf_op jit(solution)/shard_map/psum | solution.py:57
  407.8 173.3 %reduce-scatter.6.cloned.1.call-start = ((), (), s32[]{:S(2)}) async-start(), calls=%async_computation.10 | async-start | bytes 3145728 | tf_op jit(solution)/shard_map/reduce_scatter | solution.py:58
  411.1 230.1 %all-reduce.18.cloned.1.call-start = ((), (), s32[]{:S(2)}) async-start(), calls=%async_computation.13 | async-start | bytes 2097152 | tf_op jit(solution)/shard_map/psum | solution.py:12
  434.4 1.0 copy-start.5
  590.1 105.1 %all-gather.5.cloned.1.call-start = ((), (), s32[]{:S(2)}) async-start(), calls=%async_computation.14 | async-start | bytes 5242880 | tf_op jit(solution)/shard_map/all_gather | solution.py:69
  641.2 55.7 %copy-start.4 = (f32[1024,256]{1,0:T(8,128)S(1)}, f32[1024,256]{1,0:T(8,128)}, u32[]{:S(2)}) copy-start(f32[1024,256]{1,0:T(8,128)} %all-reduce.18.cloned.1.call-done) | copy-start | bytes 3145732
  641.2 75.9 %reduce-scatter.8.cloned.1.call-start = ((), (), s32[]{:S(2)}) async-start(), calls=%async_computation.15 | async-start | bytes 6291456 | tf_op jit(solution)/shard_map/reduce_scatter | solution.py:79
  695.2 2.5 copy-start.2
Sparse Core Ops, SparseCore 0:
  15.0 52.2 all-reduce.7
  69.7 21.2 all-reduce.9
  93.8 10.8 reduce-scatter.3
  240.8 50.9 all-reduce.11
  293.5 52.2 all-gather.2
  355.3 52.4 all-reduce.13
  410.2 21.2 all-reduce.15
  434.2 10.7 reduce-scatter.5
  590.2 50.9 all-reduce.17
  642.9 52.2 all-gather.4
  703.4 13.6 reduce-scatter.7
where the time goes:
time: 738 us; the launch traced here: 727 us
  waiting for transfers between devices  368 us (50%)
  other arithmetic  247 us (33%)
  local copies, waits for them, and re-layouts  49.1 us (7%)
  matrix products  32.6 us (4%)
  between operations  20 us (3%)
  blocking collectives  9.95 us (1%)
    psum x4, waiting for transfers between devices, broadcast(): return lax.psum(kept, axis)  207 us
    another operation x29, other arithmetic, block_inverse(): lower_diag = jnp.linalg.cholesky(diagonal)  158 us
    all_gather x2, waiting for transfers between devices, per_device(): gathered = lax.all_gather(panel_rows, 'row', axis=0, tiled=True)  108 us
    another operation x5, other arithmetic, block_inverse(): jax.scipy.linalg.solve_triangular(lower_diag, identity_block, lower=True)  80.1 us
    psum x2, waiting for transfers between devices, per_device(): diagonal = lax.psum(layer_diag, 'depth')  40.2 us
    another operation x27, local copies, waits for them, and re-layouts, block_inverse(): jax.scipy.linalg.solve_triangular(lower_diag, identity_block, lower=True)  19.7 us
  transfers between devices with their start and end apart: 11, of which 9 were waited for; matrix products, arithmetic and copies ran while one was open for 40% of the time, Pallas kernels for 0%

commit v1 on v0

v1 whole, which is shorter than its diff:
```python
import functools

import jax
import jax.numpy as jnp
from jax import lax
from jax.experimental import pallas as pl
from jax.experimental.pallas import tpu as pltpu
from jax.sharding import PartitionSpec as P

PANEL = 512
PANELS = 2
INNER = 128
STRIP = 8
HIGH = lax.Precision.HIGH
HIGHEST = lax.Precision.HIGHEST


def dot(a, b, ca, cb, precision):
    return lax.dot_general(
        a, b, (((ca,), (cb,)), ((), ())), precision=precision, preferred_element_type=jnp.float32
    )


def factor_strip(work, inv, strip):
    first = pl.multiple_of(strip * STRIP, STRIP)
    rows = work[pl.ds(first, STRIP), :]
    irows = inv[pl.ds(first, STRIP), :]
    rolled = pltpu.roll(rows, (INNER - first) % INNER, 1)
    sub = lax.broadcasted_iota(jnp.int32, (STRIP, INNER), 0)
    lane = lax.broadcasted_iota(jnp.int32, (STRIP, INNER), 1)
    cols = [jnp.broadcast_to(rolled[:, t : t + 1], (STRIP, INNER)) for t in range(STRIP)]
    pivots = jnp.zeros((STRIP, INNER), jnp.float32)
    for t in range(STRIP):
        pivot = jnp.broadcast_to(cols[t][t : t + 1, :], (STRIP, INNER))
        pivots = jnp.where(sub == t, pivot, pivots)
        if t + 1 < STRIP:
            mult = jnp.where(sub > t, cols[t] * (1.0 / pivot), 0.0)
            for s in range(t + 1, STRIP):
                cols[s] = cols[s] - mult * jnp.broadcast_to(cols[s][t : t + 1, :], (STRIP, INNER))
            rows = rows - mult * jnp.broadcast_to(rows[t : t + 1, :], (STRIP, INNER))
            irows = irows - mult * jnp.broadcast_to(irows[t : t + 1, :], (STRIP, INNER))
    scale = lax.rsqrt(pivots)
    rows = rows * scale
    irows = irows * scale
    inv[pl.ds(first, STRIP), :] = irows
    below = jnp.where(lane >= first + STRIP, rows, 0.0)
    update = dot(below, jnp.concatenate([rows, irows], axis=1), 0, 0, HIGHEST)
    work[...] -= update[:, :INNER]
    inv[...] -= update[:, INNER:]


def inverse_kernel(block_ref, out_ref, whole, work, inv):
    size = block_ref.shape[0]
    whole[...] = block_ref[...]
    eye = (
        lax.broadcasted_iota(jnp.int32, (INNER, INNER), 0)
        == lax.broadcasted_iota(jnp.int32, (INNER, INNER), 1)
    ).astype(jnp.float32)
    out_ref[...] = jnp.zeros_like(out_ref)
    for k in range(size // INNER):
        lo, hi = k * INNER, (k + 1) * INNER
        work[...] = whole[lo:hi, lo:hi]
        inv[...] = eye

        def step(strip, carry):
            factor_strip(work, inv, strip)
            return carry

        lax.fori_loop(0, INNER // STRIP, step, 0)
        corner = inv[...]
        if k:
            out_ref[lo:hi, :lo] = dot(corner, out_ref[lo:hi, :lo], 1, 0, HIGHEST)
        out_ref[lo:hi, lo:hi] = corner
        if hi < size:
            below = dot(whole[hi:, lo:hi], corner, 1, 1, HIGHEST)
            whole[hi:, hi:] -= dot(below, below, 1, 1, HIGHEST)
            out_ref[hi:, :hi] -= dot(below, out_ref[lo:hi, :hi], 1, 0, HIGHEST)


def block_inverse(block):
    size = block.shape[0]
    return pl.pallas_call(
        inverse_kernel,
        out_shape=jax.ShapeDtypeStruct((size, size), jnp.float32),
        in_specs=[pl.BlockSpec(memory_space=pltpu.VMEM)],
        out_specs=pl.BlockSpec(memory_space=pltpu.VMEM),
        scratch_shapes=[
            pltpu.VMEM((size, size), jnp.float32),
            pltpu.VMEM((INNER, INNER), jnp.float32),
            pltpu.VMEM((INNER, INNER), jnp.float32),
        ],
        cost_estimate=pl.CostEstimate(flops=2 * size**3, bytes_accessed=8 * size**2, transcendentals=size),
        name="block_inverse",
    )(block)


def pick(index, table):
    value = 0
    for i, entry in enumerate(table):
        value = value + jnp.where(index == i, entry, 0)
    return value


def spread_kernel(groups, s_ref, rowp, colp, diag, zrecv, zsend, rrecv, rsend, srecv, ssend, lsem):
    row_groups, col_groups = groups
    r, c, d = lax.axis_index("row"), lax.axis_index("col"), lax.axis_index("depth")
    z_chunks, chunks = zrecv.shape[1], rrecv.shape[1]
    ring = list(range(row_groups))
    if row_groups & (row_groups - 1) == 0:
        ring = [i ^ (i >> 1) for i in ring]
    place = [ring.index(i) for i in range(row_groups)]
    pos = pick(r, place)
    after = pick(r, [ring[(place[i] + 1) % row_groups] for i in range(row_groups)])
    before = pick(r, [ring[(place[i] - 1) % row_groups] for i in range(row_groups)])
    target = jnp.where(d == 0, after, before)
    half = PANEL // 2
    last = []

    def local(src, dst):
        copy = pltpu.make_async_copy(src, dst, lsem)
        copy.start()
        copy.wait()

    def line(p, k):
        root, lane = p % col_groups, (p // col_groups) * PANEL
        size = PANEL // z_chunks
        rows = pl.ds(k * size, size)
        block = rowp.at[p, rows]

        def copy(way):
            return pltpu.make_async_remote_copy(
                src_ref=block,
                dst_ref=block,
                send_sem=zsend.at[p, k, max(way, 0)],
                recv_sem=zrecv.at[p, k],
                device_id={"col": c + way},
                device_id_type=pl.DeviceIdType.MESH,
            )

        @pl.when(c == root)
        def _():
            local(s_ref.at[rows, pl.ds(lane, PANEL)], block)

        @pl.when(c != root)
        def _():
            copy(1).wait_recv()

        up, down = (c >= root) & (c < col_groups - 1), (c <= root) & (c > 0)

        @pl.when(up)
        def _():
            copy(1).start()

        @pl.when(down)
        def _():
            copy(-1).start()

        def finish():
            @pl.when(up)
            def _():
                copy(1).wait_send()

            @pl.when(down)
            def _():
                copy(-1).wait_send()

        last.append(finish)

    def around(item, root, owner, src, dst, k):
        start = place[root]
        rel = jnp.where(d == 0, (pos - start + row_groups) % row_groups, (start - pos + row_groups) % row_groups)
        size = half // chunks
        own = pl.ds(pl.multiple_of(d * half + k * size, size), size)
        other = pl.ds(pl.multiple_of((1 - d) * half + k * size, size), size)
        is_root = rel == 0
        sends = rel < row_groups - 1
        origin = is_root & (d == owner)

        def hop():
            return pltpu.make_async_remote_copy(
                src_ref=dst.at[own],
                dst_ref=dst.at[own],
                send_sem=rsend.at[item, k],
                recv_sem=rrecv.at[item, k],
                device_id={"row": target},
                device_id_type=pl.DeviceIdType.MESH,
            )

        def across(kind):
            block = dst.at[(own, other)[kind]]
            return pltpu.make_async_remote_copy(
                src_ref=block,
                dst_ref=block,
                send_sem=ssend.at[item, kind, k],
                recv_sem=srecv.at[item, kind, k],
                device_id={"depth": 1 - d},
                device_id_type=pl.DeviceIdType.MESH,
            )

        @pl.when(origin)
        def _():
            local(src.at[other], dst.at[other])
            across(1).start()
            local(src.at[own], dst.at[own])
            across(0).start()

        @pl.when(is_root & (d != owner))
        def _():
            across(1).wait_recv()

        @pl.when(rel > 0)
        def _():
            hop().wait_recv()

        @pl.when(sends)
        def _():
            hop().start()

        @pl.when(rel > 0)
        def _():
            across(0).start()

        def finish():
            @pl.when(origin)
            def _():
                across(1).wait_send()
                across(0).wait_send()

            @pl.when(jnp.logical_not(origin))
            def _():
                across(0).wait_recv()

            @pl.when(rel > 0)
            def _():
                across(0).wait_send()

            @pl.when(sends)
            def _():
                hop().wait_send()

        last.append(finish)

    def owner_of(p):
        return p % row_groups, p // row_groups

    pairs = [(p, q) for p in range(PANELS) for q in range(p + 1)]
    order = [k for j in range(z_chunks // 2) for k in (j, j + z_chunks // 2)]
    for p in range(PANELS):
        for j in range(max(z_chunks, chunks)):
            if j < z_chunks:
                line(p, order[j])
            if j < chunks:
                around(len(pairs) + p, *owner_of(p), s_ref, colp.at[p], j)
        for item, (a, b) in enumerate(pairs):
            if b == p:
                for k in range(chunks):
                    around(item, *owner_of(a), rowp.at[b], diag.at[item], k)
    for finish in last:
        finish()


def spread(summed, row_groups, col_groups):
    cols = summed.shape[1]
    z_chunks, chunks = 4, 4
    blocks = PANELS * (PANELS + 1) // 2
    items = blocks + PANELS
    dma = pltpu.SemaphoreType.DMA
    vmem = pl.BlockSpec(memory_space=pltpu.VMEM)
    return pl.pallas_call(
        functools.partial(spread_kernel, (row_groups, col_groups)),
        out_shape=(
            jax.ShapeDtypeStruct((PANELS, PANEL, PANEL), jnp.float32),
            jax.ShapeDtypeStruct((PANELS, PANEL, cols), jnp.float32),
            jax.ShapeDtypeStruct((blocks, PANEL, PANEL), jnp.float32),
        ),
        in_specs=[vmem],
        out_specs=(vmem, vmem, vmem),
        scratch_shapes=[
            dma((PANELS, z_chunks)),
            dma((PANELS, z_chunks, 2)),
            dma((items, chunks)),
            dma((items, chunks)),
            dma((items, 2, chunks)),
            dma((items, 2, chunks)),
            dma,
        ],
        compiler_params=pltpu.CompilerParams(has_side_effects=True, vmem_limit_bytes=60 * 1024 * 1024),
        name="spread",
    )(summed)


def per_device(layers):
    row_groups = lax.axis_size("row")
    col_groups = lax.axis_size("col")
    depth_groups = lax.axis_size("depth")
    row = lax.axis_index("row")
    col = lax.axis_index("col")
    depth = lax.axis_index("depth")
    layer = layers[0]
    cols_local = layer.shape[1]
    assert layer.shape[0] == PANEL * depth_groups and depth_groups == 2

    swap = [(0, 1), (1, 0)]
    mine = lax.dynamic_slice_in_dim(layer, depth * PANEL, PANEL, 0)
    theirs = lax.dynamic_slice_in_dim(layer, (1 - depth) * PANEL, PANEL, 0)
    summed = mine + lax.ppermute(theirs, "depth", swap)
    own_block = row + row_groups * depth
    col_block = jnp.arange(cols_local, dtype=jnp.int32) // PANEL * col_groups + col

    rowp, colp, diag = spread(summed, row_groups, col_groups)
    rows = [rowp[p] for p in range(PANELS)]
    cols = [colp[p] for p in range(PANELS)]
    pairs = [(p, q) for p in range(PANELS) for q in range(p + 1)]
    lead = {pair: diag[i] for i, pair in enumerate(pairs)}
    factors, left, right = [], [], []
    for p in range(PANELS):
        inverse = block_inverse(lead[p, p])
        solved = {a: dot(lead[a, p], inverse, 1, 1, HIGHEST) for a in range(p + 1, PANELS)}
        for a in range(p + 1, PANELS):
            for b in range(p + 1, a + 1):
                lead[a, b] = lead[a, b] - dot(solved[a], solved[b], 1, 1, HIGHEST)
        c_rows = jnp.where(own_block >= p, dot(rows[p], inverse, 1, 1, HIGH), 0.0)
        below = jnp.where(own_block > p, c_rows, 0.0)
        c_cols = dot(inverse, cols[p], 1, 0, HIGH)
        c_cols = jnp.where((col_block > p)[None, :], c_cols, 0.0)
        factors.append(c_rows)
        left.append(below)
        right.append(c_cols)
        for q in range(p + 1, PANELS):
            rows[q] = rows[q] - dot(below, solved[q], 1, 1, HIGH)
            cols[q] = cols[q] - dot(solved[q], c_cols, 1, 0, HIGH)
    update = dot(jnp.concatenate(left, 1), jnp.concatenate(right, 0), 1, 0, HIGH)
    schur = summed - update
    factor = jnp.stack(factors)
    width = PANEL // depth_groups
    kept = lax.dynamic_slice_in_dim(factor, depth * width, width, 2)
    sent = lax.dynamic_slice_in_dim(factor, (1 - depth) * width, width, 2)
    got = lax.ppermute(sent, "depth", swap)
    first = jnp.where(depth == 0, kept, got)
    second = jnp.where(depth == 0, got, kept)
    return jnp.concatenate([first, second], axis=1), schur


def solution(mesh):
    return jax.shard_map(
        per_device,
        mesh=mesh,
        in_specs=(P("depth", "row", "col"),),
        out_specs=(P(None, "row", "depth"), P(("row", "depth"), "col")),
        check_vma=False,
    )
```

time: 738 us -> 231 us (0.31); the launches traced: 727 us -> 230 us
  waiting for transfers between devices: 368 us -> 3.98 us
  other arithmetic: 247 us -> 5.13 us
  Pallas kernels: 0 us -> 190 us
  local copies, waits for them, and re-layouts: 49.1 us -> 6.88 us
  between operations: 20 us -> 0.75 us
  blocking collectives: 9.95 us -> 0 us
  matrix products: 32.6 us -> 22.8 us
    psum x6 -> x0, waiting for transfers between devices: 247 us -> none  [the longest x4 207 us: broadcast(): return lax.psum(kept, axis)]
    another operation x35 -> x1, other arithmetic: 240 us -> 0.11 us  [per_device(): factor = jnp.stack(factors)]
    pallas_call x0 -> x3, Pallas kernels: none -> 190 us  [the longest x1 107 us: spread(): pl.pallas_call(functools.partial(spread_kernel, (row_groups, col_groups))...]
    all_gather x2 -> x0, waiting for transfers between devices: 108 us -> none  [per_device(): gathered = lax.all_gather(panel_rows, 'row', axis=0, tiled=True)]
    another operation x35 -> x0, local copies, waits for them, and re-layouts: 20 us -> none  [the longest x27 19.7 us: block_inverse(): jax.scipy.linalg.solve_triangular(lower_diag, identity_block, lower=True)]
    another operation x26 -> x0, matrix products: 17.1 us -> none  [the longest x14 9.72 us: block_inverse(): jax.scipy.linalg.solve_triangular(lower_diag, identity_block, lower=True)]
    reduce_scatter x3 -> x0, waiting for transfers between devices: 12.4 us -> none  [the longest x1 12.4 us: per_device(): lax.psum_scatter(layer_part - outer_update(update_rows, update_cols), 'de...]
    unnamed x16 -> x10, local copies, waits for them, and re-layouts: 12.8 us -> 1.45 us
  transfers between devices with their start and end apart: 11 -> 2, of which waited for: 9 -> 1; matrix products, arithmetic and copies ran while one was open for 40% -> 5% of each run, Pallas kernels for 0% -> 0%
where the time goes in v1:
time: 231 us; the launch traced here: 230 us
  Pallas kernels  190 us (82%)
  matrix products  22.8 us (10%)
  local copies, waits for them, and re-layouts  6.88 us (3%)
  other arithmetic  5.13 us (2%)
  waiting for transfers between devices  3.98 us (2%)
    pallas_call x1, Pallas kernels, spread(): pl.pallas_call(functools.partial(spread_kernel, (row_groups, col_groups))...  107 us
    pallas_call x2, Pallas kernels, block_inverse(): pl.pallas_call(inverse_kernel, out_shape=jax.ShapeDtypeStruct((size, size...  82.8 us
    dot_general x9, matrix products, dot(): lax.dot_general(a, b, (((ca,), (cb,)), ((), ())), precision=precision, pr...  22.8 us
  transfers between devices with their start and end apart: 2, of which 1 were waited for; matrix products, arithmetic and copies ran while one was open for 5% of the time, Pallas kernels for 0%

profile of v1, /device:TPU:31, one launch (start us, length us, event | category | flops | bytes accessed | tf_op | source)
XLA Modules:
  0.0 230.1 jit_solution(9702583718136801394)
XLA Ops:
  0.6 3.2 %dynamic-slice_bitcast_fusion = f32[512,1024]{1,0:T(8,128)} fusion(f32[1,1024,1024]{2,1,0:T(8,128)} %param.1, s32[]{:T(128)S(6)} %select_n.72), kind=kLoop, calls=%fused_computation.19 | loop fusion | bytes 4194308 | tf_op jit(solution)/shard_map/dynamic_slice | solution.py:305
  3.8 0.7 collective-permute-start
  4.5 4.0 %collective-permute-done = f32[512,1024]{1,0:T(8,128)S(1)} collective-permute-done((f32[512,1024]{1,0:T(8,128)}, f32[512,1024]{1,0:T(8,128)S(1)}, u32[]{:S(2)}, u32[]{:S(2)}) %collective-permute-start) | collective-permute-done | bytes 2097184 | tf_op jit(solution)/shard_map/ppermute | solution.py:306
  8.5 3.3 %bitcast_add_fusion.s_ref = f32[512,1024]{1,0:T(8,128)} fusion(f32[512,1024]{1,0:T(8,128)S(1)} %collective-permute-done, f32[1,1024,1024]{2,1,0:T(8,128)} %param.1, s32[]{:T(128)S(6)} %select_n.71), kind=kLoop, calls=%fused_computation.16 | loop fusion | flops 524288 | bytes 6291460 | tf_op jit(solution)/shard_map/add | solution.py:306
  11.8 106.8 %spread.1 = (f32[2,512,512]{2,1,0:T(8,128)}, f32[2,512,1024]{2,1,0:T(8,128)}, f32[3,512,512]{2,1,0:T(8,128)}) custom-call(f32[512,1024]{1,0:T(8,128)} %bitcast_add_fusion.s_ref), custom_call_target="tpu_custom_call" | custom-call | tf_op jit(solution)/shard_map/spread/pallas_call | solution.py:269
  118.5 2.3 slice_bitcast_fusion.block_ref
  120.8 41.2 %block_inverse.2 = f32[512,512]{1,0:T(8,128)} custom-call(f32[512,512]{1,0:T(8,128)} %slice_bitcast_fusion.block_ref), custom_call_target="tpu_custom_call" | custom-call | flops 268435456 | bytes 2097152 | tf_op jit(solution)/shard_map/block_inverse/pallas_call | solution.py:82
  162.1 3.4 %fusion.18 = f32[512,512]{1,0:T(8,128)S(1)} fusion(f32[512,512]{1,0:T(8,128)} %block_inverse.2, f32[3,512,512]{2,1,0:T(8,128)} %get-tuple-element.6), kind=kOutput, calls=%fused_computation.27 | convolution fusion | flops 1610612736 | bytes 3145728 | tf_op jit(solution)/shard_map/dot_general | solution.py:19
  165.5 4.1 %bitcast_subtract_fusion.4.block_ref = f32[512,512]{1,0:T(8,128)} fusion(f32[3,512,512]{2,1,0:T(8,128)} %get-tuple-element.6, f32[512,512]{1,0:T(8,128)S(1)} %fusion.18), kind=kOutput, calls=%fused_computation.26 | convolution fusion | flops 1610874880 | bytes 4194304 | tf_op jit(solution)/shard_map/dot_general | solution.py:19
  169.5 41.5 %block_inverse.3 = f32[512,512]{1,0:T(8,128)} custom-call(f32[512,512]{1,0:T(8,128)} %bitcast_subtract_fusion.4.block_ref), custom_call_target="tpu_custom_call" | custom-call | flops 268435456 | bytes 2097152 | tf_op jit(solution)/shard_map/block_inverse/pallas_call | solution.py:82
  211.0 2.3 broadcast_select_fusion.1
  213.3 1.0 fusion.37
  214.4 0.2 copy-done.2
  214.5 0.7 copy-done.4
  215.2 1.1 broadcast_select_fusion
  216.3 0.1 fusion.16
  216.4 0.4 collective-permute-start.1
  216.8 0.6 copy-done.3
  217.4 1.9 fusion.12
  219.4 2.0 fusion.38
  221.4 1.9 fusion.15
  223.2 5.2 %fusion.24 = f32[512,1024]{1,0:T(8,128)} fusion(f32[512,1024]{1,0:T(8,128)S(1)} %copy-done, f32[512,1024]{1,0:T(8,128)S(1)} %fusion.15, f32[512,1024]{1,0:T(8,128)S(1)} %fusion.12, f32[512,512]{1,0:T(8,128)S(1)} %get-tuple-element.12, f32[512,512]{1,0:T(8,128)S(1)} %get-tuple-element.10), kind=kOutput, calls=%fused_computation.35 | convolution fusion | flops 3223322624 | bytes 10485760 | tf_op jit(solution)/shard_map/dot_general | solution.py:19
  228.4 0.2 broadcast_select_fusion.3
  228.7 1.5 pad_maximum_fusion
  (10 shorter events, 0.0 us)
Async XLA Ops:
  3.8 4.7 %collective-permute-start = (f32[512,1024]{1,0:T(8,128)}, f32[512,1024]{1,0:T(8,128)S(1)}, u32[]{:S(2)}, u32[]{:S(2)}) collective-permute-start(f32[512,1024]{1,0:T(8,128)} %dynamic-slice_bitcast_fusion), channel_id=1, source_target_pairs={{0,1},{1,0},{2,3},{3,2},{4,5},{5,4},{6,7},{7,6},{8,9},{9,8},{10,11... | collective-permute-start | bytes 6291464 | tf_op jit(solution)/shard_map/ppermute | solution.py:306
  169.5 41.5 %copy-start.1 = (f32[512,512]{1,0:T(8,128)S(1)}, f32[512,512]{1,0:T(8,128)}, u32[]{:S(2)}) copy-start(f32[512,512]{1,0:T(8,128)} %block_inverse.2) | copy-start | bytes 3145732
  213.3 1.2 copy-start.2
  213.3 1.9 copy-start.4
  215.2 2.2 copy-start.3
  216.4 12.0 %collective-permute-start.1 = (f32[2,512,256]{2,1,0:T(8,128)S(1)}, f32[2,512,256]{2,1,0:T(8,128)S(1)}, u32[]{:S(2)}, u32[]{:S(2)}) collective-permute-start(f32[2,512,256]{2,1,0:T(8,128)S(1)} %fusion.16), channel_id=1, source_target_pairs={{0,1},{1,0},{2,3},{3,2},{4,5},{5,4},{6,7},{7,6},{8,9},{9,8},{10,11... | collective-permute-start | bytes 3145736 | tf_op jit(solution)/shard_map/ppermute | solution.py:338
  221.3 1.9 copy-start
